TPU v7x, 32 devices: a whole 2x2x4 slice. The times are simulated.
32 devices in a mesh: expert: 4 (over y, core), fsdp: 8 (over z, x).
Axes of the slice: x: 2, y: 2, z: 4, core: 2. Of those that a mesh axis runs over, the one named last changes fastest.
Arguments:
- gradients: bfloat16 [8, 3584, 1024], P('expert', 'fsdp'), may hold values from -24 to 24, as said below
- owner: int32 [4, 2], P('expert'), may hold values from 0 to 1, each once within a row
Outputs:
- updates: bfloat16 [8, 3584, 1024], P('expert', 'fsdp')
- slot_rms: float32 [4, 8], P('expert', 'fsdp')
Inputs may be any that keep to these rules, and one draw needn't show every extreme that they name: gradients are values of mean zero and unit variance times a factor per expert between 0.5 and 2 and a factor per expert and row slice between 0.5 and 2, each entry within 24 in magnitude. Each row of owner names every place 0 to 1 exactly once.
All inputs are finite; a program needn't handle non-finite values.
Results may differ from a plain program's by a relative error of at most 0.009.
Values may be sent and summed in bfloat16 or wider, within the bound.
A program may use at most 64 MiB of HBM per device.

v0:
```python
import math
import jax
import jax.numpy as jnp
from jax import lax
from jax.sharding import PartitionSpec as P

ROWS = 3584
COLS = 1024
SHARE = 4
ITERS = 3
coef_a = 3.4445
coef_b = -4.775
coef_c = 2.0315
epsilon = 1e-07


def as_sent(value):
    return jax.tree.map(lambda a: a.astype(jnp.bfloat16) if a.dtype == jnp.float32 else a, value)


def partner_2(value, axis, distance):
    mask = 2**distance
    pairs = [(source, source ^ mask) for source in range(lax.axis_size(axis))]
    return lax.ppermute(value, axis, pairs)


def select_half(stacked, bit_value):
    retained = lax.dynamic_index_in_dim(stacked, bit_value, 0, keepdims=False)
    outgoing = lax.dynamic_index_in_dim(stacked, 1 - bit_value, 0, keepdims=False)
    return (retained, outgoing)


def join_halves(own_block, theirs, bit_value):
    leading = jnp.where(bit_value == 0, own_block, theirs)
    trailing = jnp.where(bit_value == 0, theirs, own_block)
    return jnp.concatenate([leading, trailing], axis=0)


def reduce_gram(current, low_bit, high_bit):
    partial_gram = lax.dot_general(
        current, current, (((0,), (0,)), ((), ())), preferred_element_type=jnp.float32
    )
    rounded = lax.optimization_barrier(partial_gram.astype(jnp.bfloat16))
    columns = rounded.shape[1]
    retained, outgoing = select_half(rounded.reshape(2, columns // 2, columns), low_bit)
    arrived = partner_2(as_sent(outgoing), "fsdp", 0).astype(outgoing.dtype)
    pair_sum = retained.astype(jnp.float32) + arrived.astype(jnp.float32)
    retained_pair, outgoing_pair = select_half(pair_sum.reshape(2, columns // 4, columns), high_bit)
    arrived_pair = partner_2(as_sent(outgoing_pair), "fsdp", 1).astype(outgoing_pair.dtype)
    return (retained_pair + arrived_pair).astype(jnp.bfloat16)


def spread_gram(quarter, low_bit, high_bit):
    incoming = partner_2(quarter, "fsdp", 1)
    half_block = join_halves(quarter, incoming, high_bit)
    partner = partner_2(as_sent(half_block), "fsdp", 0).astype(half_block.dtype)
    return join_halves(half_block, partner, low_bit)


def body(gradients, owner):
    expert_count, local_rows, columns = gradients.shape
    fsdp_index = lax.axis_index("fsdp")
    low_bit = fsdp_index % 2
    high_bit = fsdp_index // 2 % 2
    owner_row = owner[0]
    places = jnp.arange(expert_count, dtype=jnp.int32)
    inverse = jnp.sum(
        jnp.where(owner_row[None, :] == places[:, None], places[None, :], 0), axis=1
    ).astype(jnp.int32)
    expert_sums = jnp.sum(jnp.square(gradients.astype(jnp.float32)), axis=(1, 2))
    totals = lax.psum(expert_sums, "fsdp")
    own_expert = lax.dynamic_index_in_dim(inverse, fsdp_index // SHARE, 0, keepdims=False)
    square_sum = lax.dynamic_index_in_dim(totals, own_expert, 0, keepdims=False)
    ordered = jnp.take(gradients, inverse, axis=0)
    outbound = ordered.reshape(expert_count * SHARE, local_rows // SHARE, columns)
    held = lax.all_to_all(outbound, "fsdp", split_axis=0, concat_axis=1, tiled=True)[0]
    norm_value = jnp.sqrt(square_sum)
    current = (held.astype(jnp.float32) / (norm_value + epsilon)).astype(jnp.bfloat16)
    for iteration in range(ITERS):
        quarter = reduce_gram(current, low_bit, high_bit)
        gram_full = spread_gram(quarter, low_bit, high_bit)
        squared = jnp.dot(gram_full, gram_full, preferred_element_type=jnp.float32)
        poly = (coef_b * gram_full.astype(jnp.float32) + coef_c * squared).astype(jnp.bfloat16)
        current = (
            coef_a * current.astype(jnp.float32)
            + jnp.dot(current, poly, preferred_element_type=jnp.float32)
        ).astype(jnp.bfloat16)
    update = (math.sqrt(ROWS) * current.astype(jnp.float32)).astype(jnp.bfloat16)
    returned = lax.all_to_all(update[None], "fsdp", split_axis=1, concat_axis=0, tiled=True)
    slot_order = returned.reshape(expert_count, local_rows, columns)
    updates = jnp.take(slot_order, owner_row, axis=0)
    slot_rms = (norm_value / math.sqrt(ROWS * COLS)).reshape(1, 1).astype(jnp.float32)
    return (updates, slot_rms)


def solution(mesh):
    placed = (P("expert", "fsdp", None), P("expert", None))
    return jax.shard_map(
        body,
        mesh=mesh,
        in_specs=placed,
        out_specs=(P("expert", "fsdp", None), P("expert", "fsdp")),
        check_vma=False,
    )
```

profile of v0, /device:TPU:0, one launch (start us, length us, event | category | flops | bytes accessed | tf_op | source)
XLA Modules:
  0.0 340.0 jit_solution(16962302694401268506)
XLA Ops:
  0.6 0.8 fusion.16
  1.4 0.7 compare_select_fusion
  2.1 0.7 compare_and_fusion
  2.7 2.2 gather_fusion
  4.9 1.5 broadcast_select_fusion.1
  6.4 7.3 %all-to-all-start = ((bf16[8,112,1024]{2,1,0:T(8,128)(2,1)}), bf16[8,112,1024]{2,1,0:T(8,128)(2,1)S(1)}, u32[]{:S(2)}, u32[]{:S(2)}) async-start(bf16[8,112,1024]{2,1,0:T(8,128)(2,1)} %bitcast.71), calls=%async_computation | async-start | bytes 3670016 | tf_op jit(solution)/shard_map/all_to_all | solution.py:76
  13.7 2.1 multiply_reduce_fusion
  15.7 43.7 %psum.7 = f32[2]{0:T(128)S(1)} all-reduce(f32[2]{0:T(128)S(1)} %multiply_reduce_fusion), channel_id=1, replica_groups=mesh['expert'=4,'fsdp'=8] {'fsdp'}, use_global_device_ids=true, to_apply=%region_2.4 | all-reduce | flops 2 | bytes 16 | tf_op jit(solution)/shard_map/psum | solution.py:71
  59.4 0.6 dynamic_slice.46
  62.0 0.6 dynamic_slice.47
  63.3 0.4 divide_convert_fusion
  63.7 2.4 bitcast_convert_fusion
  66.2 1.3 copy-done
  67.5 5.0 %collective-permute-start = (bf16[512,1024]{1,0:T(8,128)(2,1)S(1)}, bf16[512,1024]{1,0:T(8,128)(2,1)S(1)}, u32[]{:S(2)}, u32[]{:S(2)}) collective-permute-start(bf16[512,1024]{1,0:T(8,128)(2,1)S(1)} %dynamic-slice_bitcast_fusion.2), channel_id=1, source_target_pairs={{0,1},{1,0},{2,3},{3,2},{4,5},{5,4},{6,7},{7,6},{8,9},{9,8},{10,11... | collective-permute-start | bytes 3145736 | tf_op jit(solution)/shard_map/ppermute | solution.py:24
  72.6 19.5 %collective-permute-done = bf16[512,1024]{1,0:T(8,128)(2,1)S(1)} collective-permute-done((bf16[512,1024]{1,0:T(8,128)(2,1)S(1)}, bf16[512,1024]{1,0:T(8,128)(2,1)S(1)}, u32[]{:S(2)}, u32[]{:S(2)}) %collective-permute-start) | collective-permute-done | bytes 1048608 | tf_op jit(solution)/shard_map/ppermute | solution.py:24
  92.0 1.6 convert_add_fusion.2
  93.6 0.1 fusion.13
  93.7 3.4 collective-permute-start.1
  97.1 9.9 %collective-permute-done.1 = bf16[256,1024]{1,0:T(8,128)(2,1)S(1)} collective-permute-done((bf16[256,1024]{1,0:T(8,128)(2,1)S(1)}, bf16[256,1024]{1,0:T(8,128)(2,1)S(1)}, u32[]{:S(2)}, u32[]{:S(2)}) %collective-permute-start.1) | collective-permute-done | bytes 524320 | tf_op jit(solution)/shard_map/ppermute | solution.py:24
  107.0 0.1 fusion.12
  107.1 2.1 collective-permute-start.2
  109.2 7.2 %collective-permute-done.2 = bf16[256,1024]{1,0:T(8,128)(2,1)S(1)} collective-permute-done((bf16[256,1024]{1,0:T(8,128)(2,1)S(1)}, bf16[256,1024]{1,0:T(8,128)(2,1)S(1)}, u32[]{:S(2)}, u32[]{:S(2)}) %collective-permute-start.2) | collective-permute-done | bytes 524320 | tf_op jit(solution)/shard_map/ppermute | solution.py:24
  116.5 2.2 collective-permute-start.3
  118.7 18.2 %collective-permute-done.3 = bf16[512,1024]{1,0:T(8,128)(2,1)S(1)} collective-permute-done((bf16[512,1024]{1,0:T(8,128)(2,1)S(1)}, bf16[512,1024]{1,0:T(8,128)(2,1)S(1)}, u32[]{:S(2)}, u32[]{:S(2)}) %collective-permute-start.3) | collective-permute-done | bytes 1048608 | tf_op jit(solution)/shard_map/ppermute | solution.py:24
  136.8 0.5 broadcast_select_fusion.7
  137.4 2.5 add_convert_fusion.2
  139.9 2.1 add_convert_fusion.5
  141.9 2.4 convolution_convert_fusion.1
  144.4 1.8 collective-permute-start.4
  146.2 17.6 %collective-permute-done.4 = bf16[512,1024]{1,0:T(8,128)(2,1)S(1)} collective-permute-done((bf16[512,1024]{1,0:T(8,128)(2,1)S(1)}, bf16[512,1024]{1,0:T(8,128)(2,1)S(1)}, u32[]{:S(2)}, u32[]{:S(2)}) %collective-permute-start.4) | collective-permute-done | bytes 1048608 | tf_op jit(solution)/shard_map/ppermute | solution.py:24
  163.8 0.4 convert_add_fusion.1
  164.3 1.0 collective-permute-start.5
  165.3 13.1 %collective-permute-done.5 = bf16[256,1024]{1,0:T(8,128)(2,1)S(1)} collective-permute-done((bf16[256,1024]{1,0:T(8,128)(2,1)S(1)}, bf16[256,1024]{1,0:T(8,128)(2,1)S(1)}, u32[]{:S(2)}, u32[]{:S(2)}) %collective-permute-start.5) | collective-permute-done | bytes 524320 | tf_op jit(solution)/shard_map/ppermute | solution.py:24
  178.5 0.2 fusion.11
  178.6 1.5 collective-permute-start.6
  180.1 7.7 %collective-permute-done.6 = bf16[256,1024]{1,0:T(8,128)(2,1)S(1)} collective-permute-done((bf16[256,1024]{1,0:T(8,128)(2,1)S(1)}, bf16[256,1024]{1,0:T(8,128)(2,1)S(1)}, u32[]{:S(2)}, u32[]{:S(2)}) %collective-permute-start.6) | collective-permute-done | bytes 524320 | tf_op jit(solution)/shard_map/ppermute | solution.py:24
  188.0 1.8 collective-permute-start.7
  189.8 14.4 %collective-permute-done.7 = bf16[512,1024]{1,0:T(8,128)(2,1)S(1)} collective-permute-done((bf16[512,1024]{1,0:T(8,128)(2,1)S(1)}, bf16[512,1024]{1,0:T(8,128)(2,1)S(1)}, u32[]{:S(2)}, u32[]{:S(2)}) %collective-permute-start.7) | collective-permute-done | bytes 1048608 | tf_op jit(solution)/shard_map/ppermute | solution.py:24
  204.3 0.6 broadcast_select_fusion.5
  204.9 2.7 add_convert_fusion.1
  207.5 2.1 add_convert_fusion.4
  209.6 2.4 convolution_convert_fusion
  212.1 1.5 collective-permute-start.8
  213.7 13.9 %collective-permute-done.8 = bf16[512,1024]{1,0:T(8,128)(2,1)S(1)} collective-permute-done((bf16[512,1024]{1,0:T(8,128)(2,1)S(1)}, bf16[512,1024]{1,0:T(8,128)(2,1)S(1)}, u32[]{:S(2)}, u32[]{:S(2)}) %collective-permute-start.8) | collective-permute-done | bytes 1048608 | tf_op jit(solution)/shard_map/ppermute | solution.py:24
  227.5 0.4 convert_add_fusion
  228.0 0.7 collective-permute-start.9
  228.7 11.2 %collective-permute-done.9 = bf16[256,1024]{1,0:T(8,128)(2,1)S(1)} collective-permute-done((bf16[256,1024]{1,0:T(8,128)(2,1)S(1)}, bf16[256,1024]{1,0:T(8,128)(2,1)S(1)}, u32[]{:S(2)}, u32[]{:S(2)}) %collective-permute-start.9) | collective-permute-done | bytes 524320 | tf_op jit(solution)/shard_map/ppermute | solution.py:24
  239.9 0.2 fusion.10
  240.0 0.4 collective-permute-start.10
  240.4 8.9 %collective-permute-done.10 = bf16[256,1024]{1,0:T(8,128)(2,1)S(1)} collective-permute-done((bf16[256,1024]{1,0:T(8,128)(2,1)S(1)}, bf16[256,1024]{1,0:T(8,128)(2,1)S(1)}, u32[]{:S(2)}, u32[]{:S(2)}) %collective-permute-start.10) | collective-permute-done | bytes 524320 | tf_op jit(solution)/shard_map/ppermute | solution.py:24
  249.4 1.0 collective-permute-start.11
  250.4 13.9 %collective-permute-done.11 = bf16[512,1024]{1,0:T(8,128)(2,1)S(1)} collective-permute-done((bf16[512,1024]{1,0:T(8,128)(2,1)S(1)}, bf16[512,1024]{1,0:T(8,128)(2,1)S(1)}, u32[]{:S(2)}, u32[]{:S(2)}) %collective-permute-start.11) | collective-permute-done | bytes 1048608 | tf_op jit(solution)/shard_map/ppermute | solution.py:24
  264.3 1.5 broadcast_select_fusion.3
  265.9 7.5 %fusion.9 = bf16[1,896,1024]{2,1,0:T(8,128)(2,1)S(1)} fusion(bf16[896,1024]{1,0:T(8,128)(2,1)} %copy-done.3, bf16[512,1024]{1,0:T(8,128)(2,1)} %get-tuple-element.4, bf16[512,1024]{1,0:T(8,128)(2,1)S(1)} %get-tuple-element.3), kind=kOutput, calls=%fused_computation.26 | convolution fusion | flops 4045537280 | bytes 5767168 | tf_op jit(solution)/shard_map/dot_general | solution.py:86
  273.4 4.8 %copy.9 = bf16[1,896,1024]{2,0,1:T(2,128)(2,1)} copy(bf16[1,896,1024]{2,1,0:T(8,128)(2,1)S(1)} %fusion.9) | data formatting | bytes 3670016 | tf_op jit(solution)/shard_map/broadcast_in_dim | solution.py:89
  278.2 0.5 broadcast.84
  278.7 11.4 %reduce = bf16[896,1024]{1,0:T(8,128)(2,1)S(1)} reduce(bf16[896,1,1024]{2,1,0:T(2,128)(2,1)} %bitcast.69, bf16[]{:T(256)} %broadcast.84), dimensions={1}, to_apply=%bitcast.68.reduce_sub_computation | reduce | bytes 3670018
  290.1 3.7 %reshape.106 = bf16[8,2,57344]{2,1,0:T(2,128)(2,1)} reshape(bf16[896,1024]{1,0:T(8,128)(2,1)S(1)} %reduce) | data formatting | bytes 3670016
  293.8 3.6 %all-to-all-start.1 = ((bf16[8,2,57344]{2,1,0:T(2,128)(2,1)}), bf16[8,2,57344]{2,1,0:T(2,128)(2,1)S(1)}, u32[]{:S(2)}, u32[]{:S(2)}) async-start(bf16[8,2,57344]{2,1,0:T(2,128)(2,1)} %reshape.106), calls=%async_computation.1 | async-start | bytes 3670016 | tf_op jit(solution)/shard_map/all_to_all | solution.py:89
  297.4 29.7 %all-to-all-done.1 = bf16[8,2,57344]{2,1,0:T(2,128)(2,1)S(1)} async-done(((bf16[8,2,57344]{2,1,0:T(2,128)(2,1)}), bf16[8,2,57344]{2,1,0:T(2,128)(2,1)S(1)}, u32[]{:S(2)}, u32[]{:S(2)}) %all-to-all-start.1) | async-done | bytes 1835040 | tf_op jit(solution)/shard_map/all_to_all | solution.py:89
  327.1 4.1 %reshape.107 = bf16[896,1,1024]{2,1,0:T(2,128)(2,1)} reshape(bf16[8,2,57344]{2,1,0:T(2,128)(2,1)S(1)} %all-to-all-done.1) | data formatting | bytes 3670016
  331.2 4.0 %copy.7 = bf16[1,896,1024]{2,1,0:T(8,128)(2,1)} copy(bf16[1,896,1024]{2,0,1:T(2,128)(2,1)} %bitcast.70) | data formatting | bytes 3670016
  335.2 2.2 gather_fusion.1
  337.4 1.5 broadcast_select_fusion
  (21 shorter events, 0.8 us)
Async XLA Ops:
  6.4 56.9 %all-to-all-start = ((bf16[8,112,1024]{2,1,0:T(8,128)(2,1)}), bf16[8,112,1024]{2,1,0:T(8,128)(2,1)S(1)}, u32[]{:S(2)}, u32[]{:S(2)}) async-start(bf16[8,112,1024]{2,1,0:T(8,128)(2,1)} %bitcast.71), calls=%async_computation | async-start | bytes 3670016 | tf_op jit(solution)/shard_map/all_to_all | solution.py:76
  63.7 2.4 copy-start.1
  66.1 1.3 copy-start
  67.5 24.5 %collective-permute-start = (bf16[512,1024]{1,0:T(8,128)(2,1)S(1)}, bf16[512,1024]{1,0:T(8,128)(2,1)S(1)}, u32[]{:S(2)}, u32[]{:S(2)}) collective-permute-start(bf16[512,1024]{1,0:T(8,128)(2,1)S(1)} %dynamic-slice_bitcast_fusion.2), channel_id=1, source_target_pairs={{0,1},{1,0},{2,3},{3,2},{4,5},{5,4},{6,7},{7,6},{8,9},{9,8},{10,11... | collective-permute-start | bytes 3145736 | tf_op jit(solution)/shard_map/ppermute | solution.py:24
  93.7 13.2 %collective-permute-start.1 = (bf16[256,1024]{1,0:T(8,128)(2,1)S(1)}, bf16[256,1024]{1,0:T(8,128)(2,1)S(1)}, u32[]{:S(2)}, u32[]{:S(2)}) collective-permute-start(bf16[256,1024]{1,0:T(8,128)(2,1)S(1)} %fusion.13), channel_id=1, source_target_pairs={{0,2},{1,3},{2,0},{3,1},{4,6},{5,7},{6,4},{7,5},{8,10},{9,11},{10,... | collective-permute-start | bytes 1572872 | tf_op jit(solution)/shard_map/ppermute | solution.py:24
  107.1 9.2 %collective-permute-start.2 = (bf16[256,1024]{1,0:T(8,128)(2,1)S(1)}, bf16[256,1024]{1,0:T(8,128)(2,1)S(1)}, u32[]{:S(2)}, u32[]{:S(2)}) collective-permute-start(bf16[256,1024]{1,0:T(8,128)(2,1)S(1)} %fusion.12), channel_id=1, source_target_pairs={{0,2},{1,3},{2,0},{3,1},{4,6},{5,7},{6,4},{7,5},{8,10},{9,11},{10,... | collective-permute-start | bytes 1572872 | tf_op jit(solution)/shard_map/ppermute | solution.py:24
  116.5 20.3 %collective-permute-start.3 = (bf16[512,1024]{1,0:T(8,128)(2,1)S(1)}, bf16[512,1024]{1,0:T(8,128)(2,1)S(1)}, u32[]{:S(2)}, u32[]{:S(2)}) collective-permute-start(bf16[512,1024]{1,0:T(8,128)(2,1)S(1)} %pad_maximum_fusion), channel_id=1, source_target_pairs={{0,1},{1,0},{2,3},{3,2},{4,5},{5,4},{6,7},{7,6},{8,9},{9,8},{10,11... | collective-permute-start | bytes 3145736 | tf_op jit(solution)/shard_map/ppermute | solution.py:24
  137.4 2.5 copy-start.2
  144.4 19.4 %collective-permute-start.4 = (bf16[512,1024]{1,0:T(8,128)(2,1)S(1)}, bf16[512,1024]{1,0:T(8,128)(2,1)S(1)}, u32[]{:S(2)}, u32[]{:S(2)}) collective-permute-start(bf16[512,1024]{1,0:T(8,128)(2,1)S(1)} %dynamic-slice_bitcast_fusion.1), channel_id=1, source_target_pairs={{0,1},{1,0},{2,3},{3,2},{4,5},{5,4},{6,7},{7,6},{8,9},{9,8},{10,11... | collective-permute-start | bytes 3145736 | tf_op jit(solution)/shard_map/ppermute | solution.py:24
  164.3 14.1 %collective-permute-start.5 = (bf16[256,1024]{1,0:T(8,128)(2,1)S(1)}, bf16[256,1024]{1,0:T(8,128)(2,1)S(1)}, u32[]{:S(2)}, u32[]{:S(2)}) collective-permute-start(bf16[256,1024]{1,0:T(8,128)(2,1)S(1)} %fusion.14), channel_id=1, source_target_pairs={{0,2},{1,3},{2,0},{3,1},{4,6},{5,7},{6,4},{7,5},{8,10},{9,11},{10,... | collective-permute-start | bytes 1572872 | tf_op jit(solution)/shard_map/ppermute | solution.py:24
  178.6 9.2 %collective-permute-start.6 = (bf16[256,1024]{1,0:T(8,128)(2,1)S(1)}, bf16[256,1024]{1,0:T(8,128)(2,1)S(1)}, u32[]{:S(2)}, u32[]{:S(2)}) collective-permute-start(bf16[256,1024]{1,0:T(8,128)(2,1)S(1)} %fusion.11), channel_id=1, source_target_pairs={{0,2},{1,3},{2,0},{3,1},{4,6},{5,7},{6,4},{7,5},{8,10},{9,11},{10,... | collective-permute-start | bytes 1572872 | tf_op jit(solution)/shard_map/ppermute | solution.py:24
  188.0 16.3 %collective-permute-start.7 = (bf16[512,1024]{1,0:T(8,128)(2,1)S(1)}, bf16[512,1024]{1,0:T(8,128)(2,1)S(1)}, u32[]{:S(2)}, u32[]{:S(2)}) collective-permute-start(bf16[512,1024]{1,0:T(8,128)(2,1)S(1)} %pad_maximum_fusion.1), channel_id=1, source_target_pairs={{0,1},{1,0},{2,3},{3,2},{4,5},{5,4},{6,7},{7,6},{8,9},{9,8},{10,11... | collective-permute-start | bytes 3145736 | tf_op jit(solution)/shard_map/ppermute | solution.py:24
  209.6 2.4 copy-start.3
  212.1 15.4 %collective-permute-start.8 = (bf16[512,1024]{1,0:T(8,128)(2,1)S(1)}, bf16[512,1024]{1,0:T(8,128)(2,1)S(1)}, u32[]{:S(2)}, u32[]{:S(2)}) collective-permute-start(bf16[512,1024]{1,0:T(8,128)(2,1)S(1)} %dynamic-slice_bitcast_fusion), channel_id=1, source_target_pairs={{0,1},{1,0},{2,3},{3,2},{4,5},{5,4},{6,7},{7,6},{8,9},{9,8},{10,11... | collective-permute-start | bytes 3145736 | tf_op jit(solution)/shard_map/ppermute | solution.py:24
  228.0 11.9 %collective-permute-start.9 = (bf16[256,1024]{1,0:T(8,128)(2,1)S(1)}, bf16[256,1024]{1,0:T(8,128)(2,1)S(1)}, u32[]{:S(2)}, u32[]{:S(2)}) collective-permute-start(bf16[256,1024]{1,0:T(8,128)(2,1)S(1)} %fusion.15), channel_id=1, source_target_pairs={{0,2},{1,3},{2,0},{3,1},{4,6},{5,7},{6,4},{7,5},{8,10},{9,11},{10,... | collective-permute-start | bytes 1572872 | tf_op jit(solution)/shard_map/ppermute | solution.py:24
  240.0 9.2 %collective-permute-start.10 = (bf16[256,1024]{1,0:T(8,128)(2,1)S(1)}, bf16[256,1024]{1,0:T(8,128)(2,1)S(1)}, u32[]{:S(2)}, u32[]{:S(2)}) collective-permute-start(bf16[256,1024]{1,0:T(8,128)(2,1)S(1)} %fusion.10), channel_id=1, source_target_pairs={{0,2},{1,3},{2,0},{3,1},{4,6},{5,7},{6,4},{7,5},{8,10},{9,11},{10,... | collective-permute-start | bytes 1572872 | tf_op jit(solution)/shard_map/ppermute | solution.py:24
  249.4 14.9 %collective-permute-start.11 = (bf16[512,1024]{1,0:T(8,128)(2,1)S(1)}, bf16[512,1024]{1,0:T(8,128)(2,1)S(1)}, u32[]{:S(2)}, u32[]{:S(2)}) collective-permute-start(bf16[512,1024]{1,0:T(8,128)(2,1)S(1)} %pad_maximum_fusion.2), channel_id=1, source_target_pairs={{0,1},{1,0},{2,3},{3,2},{4,5},{5,4},{6,7},{7,6},{8,9},{9,8},{10,11... | collective-permute-start | bytes 3145736 | tf_op jit(solution)/shard_map/ppermute | solution.py:24
  293.8 33.3 %all-to-all-start.1 = ((bf16[8,2,57344]{2,1,0:T(2,128)(2,1)}), bf16[8,2,57344]{2,1,0:T(2,128)(2,1)S(1)}, u32[]{:S(2)}, u32[]{:S(2)}) async-start(bf16[8,2,57344]{2,1,0:T(2,128)(2,1)} %reshape.106), calls=%async_computation.1 | async-start | bytes 3670016 | tf_op jit(solution)/shard_map/all_to_all | solution.py:89
where the time goes:
time: 341 us; the launch traced here: 340 us
  waiting for transfers between devices  185 us (54%)
  blocking collectives  43.7 us (13%)
  starting transfers between devices  33.2 us (10%)
  other arithmetic  24.9 us (7%)
  local copies, waits for them, and re-layouts  24.4 us (7%)
  matrix products  24 us (7%)
  between operations  4.74 us (1%)
    ppermute x12, waiting for transfers between devices, partner_2(): return lax.ppermute(value, axis, pairs)  155 us
    psum x1, blocking collectives, body(): totals = lax.psum(expert_sums, 'fsdp')  43.7 us
    all_to_all x1, waiting for transfers between devices, body(): lax.all_to_all(update[None], 'fsdp', split_axis=1, concat_axis=0, tiled=T...  29.7 us
    ppermute x12, starting transfers between devices, partner_2(): return lax.ppermute(value, axis, pairs)  22.3 us
    unnamed x12, local copies, waits for them, and re-layouts  13.6 us
    dot_general x3, matrix products, body(): jnp.dot(current, poly, preferred_element_type=jnp.float32)  11.7 us
    unnamed x1, other arithmetic  11.4 us
    all_to_all x1, starting transfers between devices, body(): lax.all_to_all(outbound, 'fsdp', split_axis=0, concat_axis=1, tiled=True)[0]  7.28 us
  transfers between devices with their start and end apart: 14, of which 13 were waited for; matrix products, arithmetic and copies ran while one was open for 1% of the time, Pallas kernels for 0%

commit v1 on v0

--- a/solution.py
+++ b/solution.py
@@ -12,6 +12,14 @@
 coef_b = -4.775
 coef_c = 2.0315
 epsilon = 1e-07
+
+
+def sum_by_hops(x, axis):
+    size, total = (lax.axis_size(axis), x)
+    for far in [1 << k for k in range(size.bit_length() - 1)]:
+        route = [(i, i ^ far) for i in range(size)]
+        total = total + lax.ppermute(total, axis, route)
+    return total
 
 
 def as_sent(value):
@@ -68,7 +76,7 @@
         jnp.where(owner_row[None, :] == places[:, None], places[None, :], 0), axis=1
     ).astype(jnp.int32)
     expert_sums = jnp.sum(jnp.square(gradients.astype(jnp.float32)), axis=(1, 2))
-    totals = lax.psum(expert_sums, "fsdp")
+    totals = sum_by_hops(expert_sums, "fsdp")
     own_expert = lax.dynamic_index_in_dim(inverse, fsdp_index // SHARE, 0, keepdims=False)
     square_sum = lax.dynamic_index_in_dim(totals, own_expert, 0, keepdims=False)
     ordered = jnp.take(gradients, inverse, axis=0)

time: 341 us -> 351 us (1.029)
  waiting for transfers between devices: 185 us -> 239 us
  blocking collectives: 43.7 us -> 0 us
    psum x1 -> x0, blocking collectives: 43.7 us -> none  [body(): totals = lax.psum(expert_sums, 'fsdp')]
    ppermute x0 -> x3, waiting for transfers between devices: none -> 30.8 us  [sum_by_hops(): total = total + lax.ppermute(total, axis, route)]
    ppermute x12, waiting for transfers between devices: 155 us -> 175 us  [partner_2(): return lax.ppermute(value, axis, pairs)]
    ppermute x12, starting transfers between devices: 22.3 us -> 13.6 us  [partner_2(): return lax.ppermute(value, axis, pairs)]
    ppermute x0 -> x3, starting transfers between devices: none -> 7.25 us  [sum_by_hops(): total = total + lax.ppermute(total, axis, route)]
  transfers between devices with their start and end apart: 14 -> 17, of which waited for: 13 -> 16; matrix products, arithmetic and copies ran while one was open for 1% -> 1% of each run, Pallas kernels for 0% -> 0%
where the time goes in v1:
time: 351 us
  waiting for transfers between devices  239 us (68%)
  starting transfers between devices  34.1 us (10%)
  other arithmetic  25.1 us (7%)
  local copies, waits for them, and re-layouts  24.4 us (7%)
  matrix products  23.8 us (7%)
  between operations  4.73 us (1%)
    ppermute x12, waiting for transfers between devices, partner_2(): return lax.ppermute(value, axis, pairs)  175 us
    all_to_all x1, waiting for transfers between devices, body(): lax.all_to_all(update[None], 'fsdp', split_axis=1, concat_axis=0, tiled=T...  32.4 us
    ppermute x3, waiting for transfers between devices, sum_by_hops(): total = total + lax.ppermute(total, axis, route)  30.8 us
    unnamed x12, local copies, waits for them, and re-layouts  13.6 us
    ppermute x12, starting transfers between devices, partner_2(): return lax.ppermute(value, axis, pairs)  13.6 us
    dot_general x3, matrix products, body(): jnp.dot(current, poly, preferred_element_type=jnp.float32)  11.7 us
    unnamed x1, other arithmetic  11.4 us
    all_to_all x1, starting transfers between devices, body(): lax.all_to_all(outbound, 'fsdp', split_axis=0, concat_axis=1, tiled=True)[0]  7.28 us
  transfers between devices with their start and end apart: 17, of which 16 were waited for; matrix products, arithmetic and copies ran while one was open for 1% of the time, Pallas kernels for 0%

profile of v1, /device:TPU:0, one launch (start us, length us, event | category | flops | bytes accessed | tf_op | source)
XLA Modules:
  0.0 350.8 jit_solution(9008918139421885259)
XLA Ops:
  0.6 0.8 fusion.16
  1.4 0.7 compare_select_fusion
  2.1 0.7 compare_and_fusion
  2.7 2.2 gather_fusion
  4.9 1.5 broadcast_select_fusion.1
  6.4 7.3 %all-to-all-start = ((bf16[8,112,1024]{2,1,0:T(8,128)(2,1)}), bf16[8,112,1024]{2,1,0:T(8,128)(2,1)S(1)}, u32[]{:S(2)}, u32[]{:S(2)}) async-start(bf16[8,112,1024]{2,1,0:T(8,128)(2,1)} %bitcast.71), calls=%async_computation | async-start | bytes 3670016 | tf_op jit(solution)/shard_map/all_to_all | solution.py:84
  13.7 2.1 multiply_reduce_fusion
  15.7 2.0 collective-permute-start
  17.8 0.6 dynamic_slice.46
  20.3 8.4 %collective-permute-done = f32[2]{0:T(128)S(1)} collective-permute-done((f32[2]{0:T(128)S(1)}, f32[2]{0:T(128)S(1)}, u32[]{:S(2)}, u32[]{:S(2)}) %collective-permute-start) | collective-permute-done | bytes 40 | tf_op jit(solution)/shard_map/ppermute | solution.py:21
  28.7 1.7 collective-permute-start.1
  30.4 14.1 %collective-permute-done.1 = f32[2]{0:T(128)S(1)} collective-permute-done((f32[2]{0:T(128)S(1)}, f32[2]{0:T(128)S(1)}, u32[]{:S(2)}, u32[]{:S(2)}) %collective-permute-start.1) | collective-permute-done | bytes 40 | tf_op jit(solution)/shard_map/ppermute | solution.py:21
  44.5 3.5 %collective-permute-start.2 = (f32[2]{0:T(128)S(1)}, f32[2]{0:T(128)S(1)}, u32[]{:S(2)}, u32[]{:S(2)}) collective-permute-start(f32[2]{0:T(128)S(1)} %add.96), channel_id=1, source_target_pairs={{0,4},{1,5},{2,6},{3,7},{4,0},{5,1},{6,2},{7,3},{8,12},{9,13},{10,... | collective-permute-start | bytes 32 | tf_op jit(solution)/shard_map/ppermute | solution.py:21
  48.0 8.4 %collective-permute-done.2 = f32[2]{0:T(128)S(1)} collective-permute-done((f32[2]{0:T(128)S(1)}, f32[2]{0:T(128)S(1)}, u32[]{:S(2)}, u32[]{:S(2)}) %collective-permute-start.2) | collective-permute-done | bytes 40 | tf_op jit(solution)/shard_map/ppermute | solution.py:21
  56.4 0.6 dynamic_slice.47
  57.7 0.4 divide_convert_fusion
  58.1 2.4 bitcast_convert_fusion
  60.5 1.3 copy-done
  61.9 1.5 collective-permute-start.3
  63.5 22.4 %collective-permute-done.3 = bf16[512,1024]{1,0:T(8,128)(2,1)S(1)} collective-permute-done((bf16[512,1024]{1,0:T(8,128)(2,1)S(1)}, bf16[512,1024]{1,0:T(8,128)(2,1)S(1)}, u32[]{:S(2)}, u32[]{:S(2)}) %collective-permute-start.3) | collective-permute-done | bytes 1048608 | tf_op jit(solution)/shard_map/ppermute | solution.py:32
  85.8 1.6 convert_add_fusion.2
  87.5 0.8 collective-permute-start.4
  88.3 11.2 %collective-permute-done.4 = bf16[256,1024]{1,0:T(8,128)(2,1)S(1)} collective-permute-done((bf16[256,1024]{1,0:T(8,128)(2,1)S(1)}, bf16[256,1024]{1,0:T(8,128)(2,1)S(1)}, u32[]{:S(2)}, u32[]{:S(2)}) %collective-permute-start.4) | collective-permute-done | bytes 524320 | tf_op jit(solution)/shard_map/ppermute | solution.py:32
  99.7 1.8 collective-permute-start.5
  101.5 10.4 %collective-permute-done.5 = bf16[256,1024]{1,0:T(8,128)(2,1)S(1)} collective-permute-done((bf16[256,1024]{1,0:T(8,128)(2,1)S(1)}, bf16[256,1024]{1,0:T(8,128)(2,1)S(1)}, u32[]{:S(2)}, u32[]{:S(2)}) %collective-permute-start.5) | collective-permute-done | bytes 524320 | tf_op jit(solution)/shard_map/ppermute | solution.py:32
  112.1 0.8 collective-permute-start.6
  112.9 21.7 %collective-permute-done.6 = bf16[512,1024]{1,0:T(8,128)(2,1)S(1)} collective-permute-done((bf16[512,1024]{1,0:T(8,128)(2,1)S(1)}, bf16[512,1024]{1,0:T(8,128)(2,1)S(1)}, u32[]{:S(2)}, u32[]{:S(2)}) %collective-permute-start.6) | collective-permute-done | bytes 1048608 | tf_op jit(solution)/shard_map/ppermute | solution.py:32
  134.6 0.5 broadcast_select_fusion.7
  135.2 2.5 add_convert_fusion.2
  137.7 2.1 add_convert_fusion.5
  139.7 2.4 convolution_convert_fusion.1
  142.6 21.4 %collective-permute-done.7 = bf16[512,1024]{1,0:T(8,128)(2,1)S(1)} collective-permute-done((bf16[512,1024]{1,0:T(8,128)(2,1)S(1)}, bf16[512,1024]{1,0:T(8,128)(2,1)S(1)}, u32[]{:S(2)}, u32[]{:S(2)}) %collective-permute-start.7) | collective-permute-done | bytes 1048608 | tf_op jit(solution)/shard_map/ppermute | solution.py:32
  163.9 0.4 convert_add_fusion.1
  164.4 1.8 collective-permute-start.8
  166.2 10.1 %collective-permute-done.8 = bf16[256,1024]{1,0:T(8,128)(2,1)S(1)} collective-permute-done((bf16[256,1024]{1,0:T(8,128)(2,1)S(1)}, bf16[256,1024]{1,0:T(8,128)(2,1)S(1)}, u32[]{:S(2)}, u32[]{:S(2)}) %collective-permute-start.8) | collective-permute-done | bytes 524320 | tf_op jit(solution)/shard_map/ppermute | solution.py:32
  176.5 1.8 collective-permute-start.9
  178.3 7.4 %collective-permute-done.9 = bf16[256,1024]{1,0:T(8,128)(2,1)S(1)} collective-permute-done((bf16[256,1024]{1,0:T(8,128)(2,1)S(1)}, bf16[256,1024]{1,0:T(8,128)(2,1)S(1)}, u32[]{:S(2)}, u32[]{:S(2)}) %collective-permute-start.9) | collective-permute-done | bytes 524320 | tf_op jit(solution)/shard_map/ppermute | solution.py:32
  185.9 0.4 collective-permute-start.10
  186.3 18.5 %collective-permute-done.10 = bf16[512,1024]{1,0:T(8,128)(2,1)S(1)} collective-permute-done((bf16[512,1024]{1,0:T(8,128)(2,1)S(1)}, bf16[512,1024]{1,0:T(8,128)(2,1)S(1)}, u32[]{:S(2)}, u32[]{:S(2)}) %collective-permute-start.10) | collective-permute-done | bytes 1048608 | tf_op jit(solution)/shard_map/ppermute | solution.py:32
  204.8 0.7 broadcast_select_fusion.5
  205.5 2.5 add_convert_fusion.1
  208.0 2.1 add_convert_fusion.4
  210.1 2.4 convolution_convert_fusion
  212.6 0.4 collective-permute-start.11
  212.9 17.6 %collective-permute-done.11 = bf16[512,1024]{1,0:T(8,128)(2,1)S(1)} collective-permute-done((bf16[512,1024]{1,0:T(8,128)(2,1)S(1)}, bf16[512,1024]{1,0:T(8,128)(2,1)S(1)}, u32[]{:S(2)}, u32[]{:S(2)}) %collective-permute-start.11) | collective-permute-done | bytes 1048608 | tf_op jit(solution)/shard_map/ppermute | solution.py:32
  230.6 0.4 convert_add_fusion
  231.1 1.8 collective-permute-start.12
  232.9 12.4 %collective-permute-done.12 = bf16[256,1024]{1,0:T(8,128)(2,1)S(1)} collective-permute-done((bf16[256,1024]{1,0:T(8,128)(2,1)S(1)}, bf16[256,1024]{1,0:T(8,128)(2,1)S(1)}, u32[]{:S(2)}, u32[]{:S(2)}) %collective-permute-start.12) | collective-permute-done | bytes 524320 | tf_op jit(solution)/shard_map/ppermute | solution.py:32
  245.4 1.8 collective-permute-start.13
  247.2 7.4 %collective-permute-done.13 = bf16[256,1024]{1,0:T(8,128)(2,1)S(1)} collective-permute-done((bf16[256,1024]{1,0:T(8,128)(2,1)S(1)}, bf16[256,1024]{1,0:T(8,128)(2,1)S(1)}, u32[]{:S(2)}, u32[]{:S(2)}) %collective-permute-start.13) | collective-permute-done | bytes 524320 | tf_op jit(solution)/shard_map/ppermute | solution.py:32
  254.8 0.4 collective-permute-start.14
  255.2 14.8 %collective-permute-done.14 = bf16[512,1024]{1,0:T(8,128)(2,1)S(1)} collective-permute-done((bf16[512,1024]{1,0:T(8,128)(2,1)S(1)}, bf16[512,1024]{1,0:T(8,128)(2,1)S(1)}, u32[]{:S(2)}, u32[]{:S(2)}) %collective-permute-start.14) | collective-permute-done | bytes 1048608 | tf_op jit(solution)/shard_map/ppermute | solution.py:32
  269.9 1.6 broadcast_select_fusion.3
  271.5 7.6 %fusion.9 = bf16[1,896,1024]{2,1,0:T(8,128)(2,1)S(1)} fusion(bf16[896,1024]{1,0:T(8,128)(2,1)} %copy-done.3, bf16[512,1024]{1,0:T(8,128)(2,1)} %get-tuple-element.4, bf16[512,1024]{1,0:T(8,128)(2,1)S(1)} %get-tuple-element.3), kind=kOutput, calls=%fused_computation.26 | convolution fusion | flops 4045537280 | bytes 5767168 | tf_op jit(solution)/shard_map/dot_general | solution.py:94
  279.1 4.8 %copy.9 = bf16[1,896,1024]{2,0,1:T(2,128)(2,1)} copy(bf16[1,896,1024]{2,1,0:T(8,128)(2,1)S(1)} %fusion.9) | data formatting | bytes 3670016 | tf_op jit(solution)/shard_map/broadcast_in_dim | solution.py:97
  283.9 0.5 broadcast.84
  284.5 11.4 %reduce = bf16[896,1024]{1,0:T(8,128)(2,1)S(1)} reduce(bf16[896,1,1024]{2,1,0:T(2,128)(2,1)} %bitcast.69, bf16[]{:T(256)} %broadcast.84), dimensions={1}, to_apply=%bitcast.68.reduce_sub_computation | reduce | bytes 3670018
  295.9 3.7 %reshape.106 = bf16[8,2,57344]{2,1,0:T(2,128)(2,1)} reshape(bf16[896,1024]{1,0:T(8,128)(2,1)S(1)} %reduce) | data formatting | bytes 3670016
  299.5 6.0 %all-to-all-start.1 = ((bf16[8,2,57344]{2,1,0:T(2,128)(2,1)}), bf16[8,2,57344]{2,1,0:T(2,128)(2,1)S(1)}, u32[]{:S(2)}, u32[]{:S(2)}) async-start(bf16[8,2,57344]{2,1,0:T(2,128)(2,1)} %reshape.106), calls=%async_computation.1 | async-start | bytes 3670016 | tf_op jit(solution)/shard_map/all_to_all | solution.py:97
  305.5 32.4 %all-to-all-done.1 = bf16[8,2,57344]{2,1,0:T(2,128)(2,1)S(1)} async-done(((bf16[8,2,57344]{2,1,0:T(2,128)(2,1)}), bf16[8,2,57344]{2,1,0:T(2,128)(2,1)S(1)}, u32[]{:S(2)}, u32[]{:S(2)}) %all-to-all-start.1) | async-done | bytes 1835040 | tf_op jit(solution)/shard_map/all_to_all | solution.py:97
  337.9 4.1 %reshape.107 = bf16[896,1,1024]{2,1,0:T(2,128)(2,1)} reshape(bf16[8,2,57344]{2,1,0:T(2,128)(2,1)S(1)} %all-to-all-done.1) | data formatting | bytes 3670016
  342.0 4.0 %copy.7 = bf16[1,896,1024]{2,1,0:T(8,128)(2,1)} copy(bf16[1,896,1024]{2,0,1:T(2,128)(2,1)} %bitcast.70) | data formatting | bytes 3670016
  346.0 2.2 gather_fusion.1
  348.2 1.5 broadcast_select_fusion
  (29 shorter events, 1.7 us)
Async XLA Ops:
  6.4 51.3 %all-to-all-start = ((bf16[8,112,1024]{2,1,0:T(8,128)(2,1)}), bf16[8,112,1024]{2,1,0:T(8,128)(2,1)S(1)}, u32[]{:S(2)}, u32[]{:S(2)}) async-start(bf16[8,112,1024]{2,1,0:T(8,128)(2,1)} %bitcast.71), calls=%async_computation | async-start | bytes 3670016 | tf_op jit(solution)/shard_map/all_to_all | solution.py:84
  15.7 13.0 %collective-permute-start = (f32[2]{0:T(128)S(1)}, f32[2]{0:T(128)S(1)}, u32[]{:S(2)}, u32[]{:S(2)}) collective-permute-start(f32[2]{0:T(128)S(1)} %multiply_reduce_fusion), channel_id=1, source_target_pairs={{0,1},{1,0},{2,3},{3,2},{4,5},{5,4},{6,7},{7,6},{8,9},{9,8},{10,11... | collective-permute-start | bytes 32 | tf_op jit(solution)/shard_map/ppermute | solution.py:21
  28.7 15.8 %collective-permute-start.1 = (f32[2]{0:T(128)S(1)}, f32[2]{0:T(128)S(1)}, u32[]{:S(2)}, u32[]{:S(2)}) collective-permute-start(f32[2]{0:T(128)S(1)} %add.95), channel_id=1, source_target_pairs={{0,2},{1,3},{2,0},{3,1},{4,6},{5,7},{6,4},{7,5},{8,10},{9,11},{10,... | collective-permute-start | bytes 32 | tf_op jit(solution)/shard_map/ppermute | solution.py:21
  44.5 11.9 %collective-permute-start.2 = (f32[2]{0:T(128)S(1)}, f32[2]{0:T(128)S(1)}, u32[]{:S(2)}, u32[]{:S(2)}) collective-permute-start(f32[2]{0:T(128)S(1)} %add.96), channel_id=1, source_target_pairs={{0,4},{1,5},{2,6},{3,7},{4,0},{5,1},{6,2},{7,3},{8,12},{9,13},{10,... | collective-permute-start | bytes 32 | tf_op jit(solution)/shard_map/ppermute | solution.py:21
  58.1 2.4 copy-start.1
  60.5 1.3 copy-start
  61.9 23.9 %collective-permute-start.3 = (bf16[512,1024]{1,0:T(8,128)(2,1)S(1)}, bf16[512,1024]{1,0:T(8,128)(2,1)S(1)}, u32[]{:S(2)}, u32[]{:S(2)}) collective-permute-start(bf16[512,1024]{1,0:T(8,128)(2,1)S(1)} %dynamic-slice_bitcast_fusion.2), channel_id=1, source_target_pairs={{0,1},{1,0},{2,3},{3,2},{4,5},{5,4},{6,7},{7,6},{8,9},{9,8},{10,11... | collective-permute-start | bytes 3145736 | tf_op jit(solution)/shard_map/ppermute | solution.py:32
  87.5 12.0 %collective-permute-start.4 = (bf16[256,1024]{1,0:T(8,128)(2,1)S(1)}, bf16[256,1024]{1,0:T(8,128)(2,1)S(1)}, u32[]{:S(2)}, u32[]{:S(2)}) collective-permute-start(bf16[256,1024]{1,0:T(8,128)(2,1)S(1)} %fusion.13), channel_id=1, source_target_pairs={{0,2},{1,3},{2,0},{3,1},{4,6},{5,7},{6,4},{7,5},{8,10},{9,11},{10,... | collective-permute-start | bytes 1572872 | tf_op jit(solution)/shard_map/ppermute | solution.py:32
  99.7 12.2 %collective-permute-start.5 = (bf16[256,1024]{1,0:T(8,128)(2,1)S(1)}, bf16[256,1024]{1,0:T(8,128)(2,1)S(1)}, u32[]{:S(2)}, u32[]{:S(2)}) collective-permute-start(bf16[256,1024]{1,0:T(8,128)(2,1)S(1)} %fusion.12), channel_id=1, source_target_pairs={{0,2},{1,3},{2,0},{3,1},{4,6},{5,7},{6,4},{7,5},{8,10},{9,11},{10,... | collective-permute-start | bytes 1572872 | tf_op jit(solution)/shard_map/ppermute | solution.py:32
  112.1 22.6 %collective-permute-start.6 = (bf16[512,1024]{1,0:T(8,128)(2,1)S(1)}, bf16[512,1024]{1,0:T(8,128)(2,1)S(1)}, u32[]{:S(2)}, u32[]{:S(2)}) collective-permute-start(bf16[512,1024]{1,0:T(8,128)(2,1)S(1)} %pad_maximum_fusion), channel_id=1, source_target_pairs={{0,1},{1,0},{2,3},{3,2},{4,5},{5,4},{6,7},{7,6},{8,9},{9,8},{10,11... | collective-permute-start | bytes 3145736 | tf_op jit(solution)/shard_map/ppermute | solution.py:32
  135.2 2.5 copy-start.2
  142.2 21.7 %collective-permute-start.7 = (bf16[512,1024]{1,0:T(8,128)(2,1)S(1)}, bf16[512,1024]{1,0:T(8,128)(2,1)S(1)}, u32[]{:S(2)}, u32[]{:S(2)}) collective-permute-start(bf16[512,1024]{1,0:T(8,128)(2,1)S(1)} %dynamic-slice_bitcast_fusion.1), channel_id=1, source_target_pairs={{0,1},{1,0},{2,3},{3,2},{4,5},{5,4},{6,7},{7,6},{8,9},{9,8},{10,11... | collective-permute-start | bytes 3145736 | tf_op jit(solution)/shard_map/ppermute | solution.py:32
  164.4 11.9 %collective-permute-start.8 = (bf16[256,1024]{1,0:T(8,128)(2,1)S(1)}, bf16[256,1024]{1,0:T(8,128)(2,1)S(1)}, u32[]{:S(2)}, u32[]{:S(2)}) collective-permute-start(bf16[256,1024]{1,0:T(8,128)(2,1)S(1)} %fusion.14), channel_id=1, source_target_pairs={{0,2},{1,3},{2,0},{3,1},{4,6},{5,7},{6,4},{7,5},{8,10},{9,11},{10,... | collective-permute-start | bytes 1572872 | tf_op jit(solution)/shard_map/ppermute | solution.py:32
  176.5 9.2 %collective-permute-start.9 = (bf16[256,1024]{1,0:T(8,128)(2,1)S(1)}, bf16[256,1024]{1,0:T(8,128)(2,1)S(1)}, u32[]{:S(2)}, u32[]{:S(2)}) collective-permute-start(bf16[256,1024]{1,0:T(8,128)(2,1)S(1)} %fusion.11), channel_id=1, source_target_pairs={{0,2},{1,3},{2,0},{3,1},{4,6},{5,7},{6,4},{7,5},{8,10},{9,11},{10,... | collective-permute-start | bytes 1572872 | tf_op jit(solution)/shard_map/ppermute | solution.py:32
  185.9 18.9 %collective-permute-start.10 = (bf16[512,1024]{1,0:T(8,128)(2,1)S(1)}, bf16[512,1024]{1,0:T(8,128)(2,1)S(1)}, u32[]{:S(2)}, u32[]{:S(2)}) collective-permute-start(bf16[512,1024]{1,0:T(8,128)(2,1)S(1)} %pad_maximum_fusion.1), channel_id=1, source_target_pairs={{0,1},{1,0},{2,3},{3,2},{4,5},{5,4},{6,7},{7,6},{8,9},{9,8},{10,11... | collective-permute-start | bytes 3145736 | tf_op jit(solution)/shard_map/ppermute | solution.py:32
  210.1 2.4 copy-start.3
  212.6 18.0 %collective-permute-start.11 = (bf16[512,1024]{1,0:T(8,128)(2,1)S(1)}, bf16[512,1024]{1,0:T(8,128)(2,1)S(1)}, u32[]{:S(2)}, u32[]{:S(2)}) collective-permute-start(bf16[512,1024]{1,0:T(8,128)(2,1)S(1)} %dynamic-slice_bitcast_fusion), channel_id=1, source_target_pairs={{0,1},{1,0},{2,3},{3,2},{4,5},{5,4},{6,7},{7,6},{8,9},{9,8},{10,11... | collective-permute-start | bytes 3145736 | tf_op jit(solution)/shard_map/ppermute | solution.py:32
  231.1 14.2 %collective-permute-start.12 = (bf16[256,1024]{1,0:T(8,128)(2,1)S(1)}, bf16[256,1024]{1,0:T(8,128)(2,1)S(1)}, u32[]{:S(2)}, u32[]{:S(2)}) collective-permute-start(bf16[256,1024]{1,0:T(8,128)(2,1)S(1)} %fusion.15), channel_id=1, source_target_pairs={{0,2},{1,3},{2,0},{3,1},{4,6},{5,7},{6,4},{7,5},{8,10},{9,11},{10,... | collective-permute-start | bytes 1572872 | tf_op jit(solution)/shard_map/ppermute | solution.py:32
  245.4 9.2 %collective-permute-start.13 = (bf16[256,1024]{1,0:T(8,128)(2,1)S(1)}, bf16[256,1024]{1,0:T(8,128)(2,1)S(1)}, u32[]{:S(2)}, u32[]{:S(2)}) collective-permute-start(bf16[256,1024]{1,0:T(8,128)(2,1)S(1)} %fusion.10), channel_id=1, source_target_pairs={{0,2},{1,3},{2,0},{3,1},{4,6},{5,7},{6,4},{7,5},{8,10},{9,11},{10,... | collective-permute-start | bytes 1572872 | tf_op jit(solution)/shard_map/ppermute | solution.py:32
  254.8 15.1 %collective-permute-start.14 = (bf16[512,1024]{1,0:T(8,128)(2,1)S(1)}, bf16[512,1024]{1,0:T(8,128)(2,1)S(1)}, u32[]{:S(2)}, u32[]{:S(2)}) collective-permute-start(bf16[512,1024]{1,0:T(8,128)(2,1)S(1)} %pad_maximum_fusion.2), channel_id=1, source_target_pairs={{0,1},{1,0},{2,3},{3,2},{4,5},{5,4},{6,7},{7,6},{8,9},{9,8},{10,11... | collective-permute-start | bytes 3145736 | tf_op jit(solution)/shard_map/ppermute | solution.py:32
  299.5 38.4 %all-to-all-start.1 = ((bf16[8,2,57344]{2,1,0:T(2,128)(2,1)}), bf16[8,2,57344]{2,1,0:T(2,128)(2,1)S(1)}, u32[]{:S(2)}, u32[]{:S(2)}) async-start(bf16[8,2,57344]{2,1,0:T(2,128)(2,1)} %reshape.106), calls=%async_computation.1 | async-start | bytes 3670016 | tf_op jit(solution)/shard_map/all_to_all | solution.py:97
